TPU v7x, 32 devices: a whole 2x2x4 slice. The times are simulated.
32 devices in a mesh: dp: 2 (over x), vocab: 16 (over z, y, core).
Axes of the slice: x: 2, y: 2, z: 4, core: 2. Of those that a mesh axis runs over, the one named last changes fastest.
Arguments:
- hidden: bfloat16 [96, 8192], P('dp', 'vocab'), may hold values from -90 to 90
- weight: bfloat16 [8192, 38016], P('dp', 'vocab'), may hold values from -0.1875 to 0.1875
- targets: int32 [96], P('dp'), may hold values from 0 to 38015
- pad_mask: int32 [96], P('dp'), may hold values from 0 to 1
Outputs:
- token_nll: float32 [96], P('dp')
- nll_total: float32 [], replicated
All inputs are finite; a program needn't handle non-finite values.
Results may differ from a plain program's by a relative error of at most 0.0003.
Values may be sent and summed in bfloat16 or wider, within the bound.
No kernel may reach another device: no remote copies, remote signals or barrier semaphores. Data moves between devices by JAX's collectives and lax.ppermute only.
A program may use at most 64 MiB of HBM per device.

v0:
```python
import jax
import jax.numpy as jnp
from jax import lax
from jax.sharding import PartitionSpec as P


def merged_2(value, axis, join):
    pieces = jax.tree.map(lambda part: lax.all_gather(part, axis), value)
    head = jax.tree.map(lambda part: part[0], pieces)
    tail = jax.tree.map(lambda part: part[1:], pieces)
    subtotal, _ = lax.scan(lambda subtotal, share: (join(subtotal, share), None), head, tail)
    return subtotal


def join_stats(earlier, later):
    max_one, sum_one, pick_one = earlier
    max_two, sum_two, pick_two = later
    merged = jnp.maximum(max_one, max_two)
    return (
        merged,
        sum_one * jnp.exp(max_one - merged) + sum_two * jnp.exp(max_two - merged),
        pick_one + pick_two,
    )


def per_device(hidden, weight, targets, pad_mask):
    dp_size = lax.axis_size("dp")
    whole_width = lax.all_gather(hidden, "vocab", axis=1, tiled=True)
    tok_dev = whole_width.shape[0]
    n_cols = weight.shape[1]
    spread = lax.all_to_all(whole_width, "dp", split_axis=1, concat_axis=0, tiled=True)
    cols_sub = n_cols // dp_size
    logits = lax.psum_scatter(
        lax.dot_general(
            weight, spread, (((0,), (1,)), ((), ())), preferred_element_type=jnp.float32
        ),
        "dp",
        scatter_dimension=0,
        tiled=True,
    )
    all_targets, all_mask = (
        lax.all_gather(targets, "dp", axis=0, tiled=True),
        lax.all_gather(pad_mask, "dp", axis=0, tiled=True),
    )
    col_base = lax.axis_index("vocab") * n_cols + lax.axis_index("dp") * cols_sub
    column_ids = lax.broadcasted_iota(jnp.int32, (cols_sub, 1), 0) + col_base
    is_target = column_ids == all_targets[None, :]
    local_pick = jnp.sum(jnp.where(is_target, logits, 0.0), axis=0)
    local_max = jnp.max(logits, axis=0)
    local_sum = jnp.sum(jnp.exp(logits - local_max[None, :]), axis=0)
    row_max, exp_sum, picked = merged_2(
        (local_max, local_sum, local_pick), ("dp", "vocab"), join_stats
    )
    every_nll = all_mask.astype(jnp.float32) * (row_max + jnp.log(exp_sum) - picked)
    nll_total = jnp.sum(every_nll)
    token_nll = lax.dynamic_slice_in_dim(every_nll, lax.axis_index("dp") * tok_dev, tok_dev, 0)
    return (token_nll, nll_total)


def solution(mesh):
    placed = (P("dp", "vocab"), P("dp", "vocab"), P("dp"), P("dp"))
    return jax.shard_map(
        per_device, mesh=mesh, in_specs=placed, out_specs=(P("dp"), P()), check_vma=False
    )
```

profile of v0, /device:TPU:0, one launch (start us, length us, event | category | flops | bytes accessed | tf_op | source)
XLA Modules:
  0.0 145.3 jit_solution(8605927002165873996)
XLA Ops:
  7.2 0.0 copy-start
  7.2 0.0 copy-start.1
  7.2 0.0 copy-start.2
  7.2 0.0 all-reduce.10.cloned.1.call-start
  7.2 25.7 %all_gather.28 = bf16[48,8192]{1,0:T(8,128)(2,1)S(1)} all-gather(bf16[48,512]{1,0:T(8,128)(2,1)} %param.6), channel_id=1, replica_groups=mesh['dp'=2,'vocab'=16] {'vocab'}, dimensions={1}, use_global_device_ids=true | all-gather | bytes 835584 | tf_op jit(solution)/shard_map/all_gather | solution.py:28
  33.0 0.1 copy.12
  33.0 14.0 %all_to_all.19 = bf16[48,2,4096]{2,0,1:T(8,128)(2,1)S(1)} all-to-all(bf16[48,2,4096]{2,0,1:T(8,128)(2,1)S(1)} %bitcast.33), channel_id=1, replica_groups=mesh['dp'=2,'vocab'=16] {'dp'}, dimensions={1} | all-to-all | bytes 1572864 | tf_op jit(solution)/shard_map/all_to_all | solution.py:31
  47.0 11.1 %fusion.10 = f32[2376,96]{0,1:T(8,128)} fusion(bf16[4096,2376]{0,1:T(8,128)(2,1)} %param.7, bf16[96,4096]{1,0:T(8,128)(2,1)S(1)} %bitcast.32), kind=kOutput, calls=%fused_computation.18 | convolution fusion | flops 1868562432 | bytes 21163008 | tf_op jit(solution)/shard_map/dot_general | solution.py:34
  58.2 0.0 all-reduce.10.cloned.1.call-update
  58.2 0.0 copy-done
  58.2 0.7 fusion.9
  59.6 0.0 copy-done.1
  59.6 0.2 dynamic-update-slice
  59.8 0.0 copy-done.2
  59.8 0.2 dynamic-update-slice.3
  60.7 4.5 %all-reduce.6 = (s32[96]{0:T(128)S(1)}, s32[96]{0:T(128)S(1)}) all-reduce(s32[96]{0:T(128)S(1)} %dynamic-update-slice.3, s32[96]{0:T(128)S(1)} %dynamic-update-slice), channel_id=1, replica_groups=mesh['dp'=2,'vocab'=16] {'dp'}, use_global_device_ids=true, to_apply=%add.3 | all-reduce | flops 192 | bytes 1536
  65.2 26.8 %all-reduce.10.cloned.1.call-done = f32[2376,96]{0,1:T(8,128)} async-done(((f32[2376,96]{0,1:T(8,128)}), f32[2376,96]{0,1:T(8,128)}) %all-reduce.10.cloned.1.call-update) | async-done | bytes 912400
  92.0 1.3 dynamic-slice_reduce_fusion
  93.4 0.3 dynamic-update-slice.1
  93.7 1.4 select_reduce_fusion
  95.1 0.3 dynamic-update-slice.4
  95.3 0.3 dynamic-update-slice.2
  95.6 39.9 %all-reduce.7 = (f32[3072]{0:T(1024)S(1)}, f32[3072]{0:T(1024)S(1)}, f32[3072]{0:T(1024)S(1)}) all-reduce(f32[3072]{0:T(1024)S(1)} %dynamic-update-slice.1, f32[3072]{0:T(1024)S(1)} %dynamic-update-slice.2, f32[3072]{0:T(1024)S(1)} %dynamic-update-slice.4), channel_id=2, replica_groups=mesh['dp'=2,'vocab'=16] {'dp','vocab'}, use_global_device_ids=true, to_apply=%add.1 | all-reduce | flops 9216 | bytes 73728
  135.5 0.1 slice.33
  135.6 0.1 slice.34
  135.6 0.1 slice.35
  135.7 0.1 reshape.23
  135.8 0.1 reshape.24
  135.9 0.1 reshape.25
  135.9 1.4 while.14
  137.3 0.6 fusion.8
  137.9 0.6 dynamic_slice.13
  (40 shorter events, 1.0 us)
Async XLA Ops:
  7.2 51.1 %copy-start = (u32[32]{0:T(128)S(1)}, u32[32]{0:T(128)}, u32[]{:S(2)}) copy-start(u32[32]{0:T(128)} %constant.35) | copy-start | bytes 388
  7.2 52.4 %copy-start.1 = (s32[48]{0:T(128)S(1)}, s32[48]{0:T(128)}, u32[]{:S(2)}) copy-start(s32[48]{0:T(128)} %param.9) | copy-start | bytes 580
  7.2 52.6 %copy-start.2 = (s32[48]{0:T(128)S(1)}, s32[48]{0:T(128)}, u32[]{:S(2)}) copy-start(s32[48]{0:T(128)} %param.8) | copy-start | bytes 580
  7.2 84.8 %all-reduce.10.cloned.1.call-start = ((), (), s32[]{:S(2)}) async-start(), calls=%async_computation.1 | async-start | bytes 1867776
Sparse Core Ops, SparseCore 0:
  58.3 33.6 all-reduce.9
where the time goes:
time: 146 us; the launch traced here: 145 us
  blocking collectives  84.1 us (58%)
  waiting for transfers between devices  26.8 us (18%)
  between operations  15.5 us (11%)
  matrix products  11.1 us (8%)
  other arithmetic  4.28 us (3%)
  local copies, waits for them, and re-layouts  3.04 us (2%)
    unnamed x2, blocking collectives  44.4 us
    unnamed x2, waiting for transfers between devices  26.8 us
    all_gather x1, blocking collectives, per_device(): whole_width = lax.all_gather(hidden, 'vocab', axis=1, tiled=True)  25.7 us
    all_to_all x1, blocking collectives, per_device(): lax.all_to_all(whole_width, 'dp', split_axis=1, concat_axis=0, tiled=True)  14 us
    dot_general x1, matrix products, per_device(): lax.dot_general(weight, spread, (((0,), (1,)), ((), ())), preferred_eleme...  11.1 us
  transfers between devices with their start and end apart: 1, of which 1 were waited for; matrix products, arithmetic and copies ran while one was open for 1% of the time, Pallas kernels for 0%

commit v1 on v0

--- a/solution.py
+++ b/solution.py
@@ -28,7 +28,9 @@
     whole_width = lax.all_gather(hidden, "vocab", axis=1, tiled=True)
     tok_dev = whole_width.shape[0]
     n_cols = weight.shape[1]
-    spread = lax.all_to_all(whole_width, "dp", split_axis=1, concat_axis=0, tiled=True)
+    shards = jnp.split(whole_width, lax.axis_size("dp"), axis=1)
+    received = lax.all_to_all(jnp.stack(shards), "dp", 0, 0)
+    spread = jnp.concatenate(received, axis=0)
     cols_sub = n_cols // dp_size
     logits = lax.psum_scatter(
         lax.dot_general(

time: 146 us -> 148 us (1.014)
  matrix products: 11.1 us -> 13.6 us
    dot_general x1, matrix products: 11.1 us -> 13.6 us  [per_device(): lax.dot_general(weight, spread, (((0,), (1,)), ((), ())), preferred_eleme...]
where the time goes in v1:
time: 148 us
  blocking collectives  84.1 us (57%)
  waiting for transfers between devices  26.8 us (18%)
  between operations  15.5 us (10%)
  matrix products  13.6 us (9%)
  other arithmetic  4.35 us (3%)
  local copies, waits for them, and re-layouts  3.04 us (2%)
    unnamed x2, blocking collectives  44.4 us
    unnamed x2, waiting for transfers between devices  26.8 us
    all_gather x1, blocking collectives, per_device(): whole_width = lax.all_gather(hidden, 'vocab', axis=1, tiled=True)  25.7 us
    all_to_all x1, blocking collectives, per_device(): received = lax.all_to_all(jnp.stack(shards), 'dp', 0, 0)  14 us
    dot_general x1, matrix products, per_device(): lax.dot_general(weight, spread, (((0,), (1,)), ((), ())), preferred_eleme...  13.6 us
  transfers between devices with their start and end apart: 1, of which 1 were waited for; matrix products, arithmetic and copies ran while one was open for 1% of the time, Pallas kernels for 0%

profile of v1, /device:TPU:0, one launch (start us, length us, event | category | flops | bytes accessed | tf_op | source)
XLA Modules:
  0.0 147.9 jit_solution(5381424502799600877)
XLA Ops:
  7.2 0.0 copy-start
  7.2 0.0 copy-start.1
  7.2 0.0 copy-start.2
  7.2 0.0 all-reduce.10.cloned.1.call-start
  7.2 25.7 %all_gather.28 = bf16[48,8192]{1,0:T(8,128)(2,1)S(1)} all-gather(bf16[48,512]{1,0:T(8,128)(2,1)} %param.6), channel_id=1, replica_groups=mesh['dp'=2,'vocab'=16] {'vocab'}, dimensions={1}, use_global_device_ids=true | all-gather | bytes 835584 | tf_op jit(solution)/shard_map/all_gather | solution.py:28
  33.0 0.1 slice_bitcast_fusion.1
  33.0 0.1 pad_maximum_fusion
  33.1 14.0 %all_to_all.5 = bf16[2,48,4096]{2,1,0:T(8,128)(2,1)S(1)} all-to-all(bf16[2,48,4096]{2,1,0:T(8,128)(2,1)S(1)} %pad_maximum_fusion), channel_id=1, replica_groups=mesh['dp'=2,'vocab'=16] {'dp'}, dimensions={0} | all-to-all | bytes 1572864 | tf_op jit(solution)/shard_map/all_to_all | solution.py:32
  47.1 13.6 %convolution_bitcast_fusion = f32[2376,96]{0,1:T(8,128)} fusion(bf16[96,4096]{1,0:T(8,128)(2,1)S(1)} %bitcast.32, bf16[4096,2376]{0,1:T(8,128)(2,1)} %param.7), kind=kOutput, calls=%fused_computation.10 | convolution fusion | flops 1868562432 | bytes 21163008 | tf_op jit(solution)/shard_map/dot_general | solution.py:36
  60.7 0.0 all-reduce.10.cloned.1.call-update
  60.7 0.0 copy-done
  60.7 0.7 fusion.9
  62.1 0.0 copy-done.1
  62.1 0.2 dynamic-update-slice
  62.3 0.0 copy-done.2
  62.3 0.2 dynamic-update-slice.3
  63.3 4.5 %all-reduce.6 = (s32[96]{0:T(128)S(1)}, s32[96]{0:T(128)S(1)}) all-reduce(s32[96]{0:T(128)S(1)} %dynamic-update-slice.3, s32[96]{0:T(128)S(1)} %dynamic-update-slice), channel_id=1, replica_groups=mesh['dp'=2,'vocab'=16] {'dp'}, use_global_device_ids=true, to_apply=%add.3 | all-reduce | flops 192 | bytes 1536
  67.7 26.8 %all-reduce.10.cloned.1.call-done = f32[2376,96]{0,1:T(8,128)} async-done(((f32[2376,96]{0,1:T(8,128)}), f32[2376,96]{0,1:T(8,128)}) %all-reduce.10.cloned.1.call-update) | async-done | bytes 912400
  94.5 1.3 dynamic-slice_reduce_fusion
  95.9 0.3 dynamic-update-slice.1
  96.2 1.4 select_reduce_fusion
  97.6 0.3 dynamic-update-slice.4
  97.8 0.3 dynamic-update-slice.2
  98.1 39.9 %all-reduce.7 = (f32[3072]{0:T(1024)S(1)}, f32[3072]{0:T(1024)S(1)}, f32[3072]{0:T(1024)S(1)}) all-reduce(f32[3072]{0:T(1024)S(1)} %dynamic-update-slice.1, f32[3072]{0:T(1024)S(1)} %dynamic-update-slice.2, f32[3072]{0:T(1024)S(1)} %dynamic-update-slice.4), channel_id=2, replica_groups=mesh['dp'=2,'vocab'=16] {'dp','vocab'}, use_global_device_ids=true, to_apply=%add.1 | all-reduce | flops 9216 | bytes 73728
  138.0 0.1 slice.33
  138.1 0.1 slice.34
  138.2 0.1 slice.35
  138.2 0.1 reshape.24
  138.3 0.1 reshape.25
  138.4 0.1 reshape.26
  138.4 1.4 while.14
  139.8 0.6 fusion.8
  140.4 0.6 dynamic_slice.13
  (40 shorter events, 1.0 us)
Async XLA Ops:
  7.2 53.6 %copy-start = (u32[32]{0:T(128)S(1)}, u32[32]{0:T(128)}, u32[]{:S(2)}) copy-start(u32[32]{0:T(128)} %constant.35) | copy-start | bytes 388
  7.2 54.9 %copy-start.1 = (s32[48]{0:T(128)S(1)}, s32[48]{0:T(128)}, u32[]{:S(2)}) copy-start(s32[48]{0:T(128)} %param.9) | copy-start | bytes 580
  7.2 55.1 %copy-start.2 = (s32[48]{0:T(128)S(1)}, s32[48]{0:T(128)}, u32[]{:S(2)}) copy-start(s32[48]{0:T(128)} %param.8) | copy-start | bytes 580
  7.2 87.3 %all-reduce.10.cloned.1.call-start = ((), (), s32[]{:S(2)}) async-start(), calls=%async_computation.1 | async-start | bytes 1867776
Sparse Core Ops, SparseCore 0:
  60.8 33.6 all-reduce.9
